TPU v7x, 32 devices: a whole 2x2x4 slice. The times are simulated.
32 devices in a mesh: dp: 8 (over z, y), tp: 4 (over x, core).
Axes of the slice: x: 2, y: 2, z: 4, core: 2. Of those that a mesh axis runs over, the one named last changes fastest.
Arguments:
- q_latent: bfloat16 [1024, 4, 1536], P('dp'), may hold values from -6 to 6
- new_latent: bfloat16 [1024, 4, 512], P('dp'), may hold values from -6 to 6
- new_rope: bfloat16 [1024, 4, 64], P('dp'), may hold values from -6 to 6
- cache_latent: bfloat16 [1024, 256, 512], P('dp'), may hold values from -6 to 6
- cache_rope: bfloat16 [1024, 64, 256], P('dp'), may hold values from -1200 to 1200
- lengths: int32 [1024], P('dp'), may hold values from 1 to 256
- assignment: int32 [8, 128], P('dp'), may hold values from 0 to 127, each once within a row
- w_uq: float32 [1536, 12288], P(('dp', 'tp')), may hold values from -0.15625 to 0.15625
- w_uk: float32 [512, 8192], P(('dp', 'tp')), may hold values from -0.75 to 0.75
- w_uv: float32 [512, 8192], P(('dp', 'tp')), may hold values from -0.25 to 0.25
- w_o: float32 [8192, 7168], P(None, ('dp', 'tp')), may hold values from -0.0625 to 0.0625
Outputs:
- attention_out: bfloat16 [1024, 4, 7168], P('dp', None, 'tp')
- weight_norm: float32 [1], replicated
Inputs may be any that keep to these rules, and one draw needn't show every extreme that they name: Each row of assignment is a permutation of 0 to 127.
All inputs are finite; a program needn't handle non-finite values.
Results may differ from a plain program's by a relative error of at most 0.006.
The roundings to bfloat16 on the way count: a program that leaves them out, or rounds other values in their place, can miss the bound.
Values may be sent and summed in bfloat16 or wider, within the bound.
A program may use at most 256 MiB of HBM per device.

v0:
```python
import jax
import jax.numpy as jnp
from jax import lax
from jax.sharding import PartitionSpec as P

D = 7168
QRANK = 1536
KVRANK = 512
NOPE = 128
ROPE = 64
VDIM = 128
HEADS = 64
NEWTOK = 4
CACHE = 256


def widen(values):
    return lax.optimization_barrier(values).astype(jnp.float32)


def rotate_half(values, positions):
    half_width = values.shape[-1] // 2
    frequency = 10000.0 ** (-jnp.arange(half_width, dtype=jnp.float32) / half_width)
    angles = positions.astype(jnp.float32)[:, :, None, None] * frequency
    cosine = jnp.cos(angles)
    sine_part = jnp.sin(angles)
    lower_half = values[..., :half_width]
    upper_half = values[..., half_width:]
    return jnp.concatenate(
        [
            lower_half * cosine - upper_half * sine_part,
            upper_half * cosine + lower_half * sine_part,
        ],
        axis=-1,
    )


def shards(
    q_latent,
    new_latent,
    new_rope,
    cache_latent,
    cache_rope,
    lengths,
    assignment,
    w_uq,
    w_uk,
    w_uv,
    w_o,
):
    local_squares = (
        jnp.sum(w_uq * w_uq) + jnp.sum(w_uk * w_uk) + jnp.sum(w_uv * w_uv) + jnp.sum(w_o * w_o)
    )
    squares_total = lax.psum(local_squares, ("dp", "tp"))
    weight_norm = jnp.sqrt(squares_total / (HEADS * (NOPE + ROPE) + 2 * HEADS * NOPE + D)).reshape(
        1
    )
    query_cast = w_uq.astype(jnp.bfloat16)
    key_cast = w_uk.astype(jnp.bfloat16)
    value_cast = w_uv.astype(jnp.bfloat16)
    gathered = (
        lax.all_gather(query_cast[None], "dp", axis=0, tiled=True),
        lax.all_gather(key_cast[None], "dp", axis=0, tiled=True),
        lax.all_gather(value_cast[None], "dp", axis=0, tiled=True),
    )
    mixed = (
        lax.all_to_all(gathered[0], "tp", split_axis=2, concat_axis=1, tiled=True),
        lax.all_to_all(gathered[1], "tp", split_axis=2, concat_axis=1, tiled=True),
        lax.all_to_all(gathered[2], "tp", split_axis=2, concat_axis=1, tiled=True),
    )
    query_up = mixed[0].reshape(-1, mixed[0].shape[2])
    key_up = mixed[1].reshape(-1, mixed[1].shape[2])
    value_up = mixed[2].reshape(-1, mixed[2].shape[2])
    out_cast = w_o.astype(jnp.bfloat16)
    seq_count = q_latent.shape[0]
    heads_here = key_up.shape[1] // NOPE
    selector = (assignment[0][:, None] == jnp.arange(seq_count, dtype=jnp.int32)[None, :]).astype(
        jnp.bfloat16
    )

    def to_slots(array):
        moved = jnp.dot(
            selector.T, array.reshape(seq_count, -1), preferred_element_type=jnp.float32
        )
        return moved.astype(jnp.bfloat16).reshape(array.shape)

    query_slots = to_slots(q_latent)
    latent_slots = to_slots(new_latent)
    rope_slots = to_slots(new_rope)
    projected = jnp.dot(
        query_slots.reshape(seq_count * NEWTOK, QRANK), query_up, preferred_element_type=jnp.float32
    )
    projected = projected.astype(jnp.bfloat16).reshape(seq_count, NEWTOK, heads_here, NOPE + ROPE)
    query_nope = projected[..., :NOPE]
    positions = lengths[:, None] + jnp.arange(NEWTOK, dtype=jnp.int32)[None, :]
    query_rot = rotate_half(widen(projected[..., NOPE:]), positions).astype(jnp.bfloat16)
    absorbed = jnp.einsum(
        "sqhn,chn->sqhc",
        query_nope,
        key_up.reshape(KVRANK, heads_here, NOPE),
        preferred_element_type=jnp.float32,
    ).astype(jnp.bfloat16)
    scale = (NOPE + ROPE) ** (-0.5)
    cache_scores = jnp.einsum(
        "sqhc,stc->sqht", absorbed, cache_latent, preferred_element_type=jnp.float32
    )
    cache_scores = (
        cache_scores
        + jnp.einsum("sqhr,srt->sqht", query_rot, cache_rope, preferred_element_type=jnp.float32)
    ) * scale
    valid = jnp.arange(CACHE, dtype=jnp.int32)[None, :] < lengths[:, None]
    cache_scores = jnp.where(valid[:, None, None, :], cache_scores, -jnp.inf)
    new_scores = jnp.einsum(
        "sqhc,skc->sqhk", absorbed, latent_slots, preferred_element_type=jnp.float32
    )
    new_scores = (
        new_scores
        + jnp.einsum("sqhr,skr->sqhk", query_rot, rope_slots, preferred_element_type=jnp.float32)
    ) * scale
    causal = jnp.arange(NEWTOK)[:, None] >= jnp.arange(NEWTOK)[None, :]
    new_scores = jnp.where(causal[None, :, None, :], new_scores, -jnp.inf)
    scores = jnp.concatenate([cache_scores, new_scores], axis=-1)
    largest = jnp.max(scores, axis=-1, keepdims=True)
    expo = jnp.exp(scores - largest)
    weights = (expo / jnp.sum(expo, axis=-1, keepdims=True)).astype(jnp.bfloat16)
    latent_out = jnp.einsum(
        "sqht,stc->sqhc", weights[..., :CACHE], cache_latent, preferred_element_type=jnp.float32
    )
    latent_out = (
        latent_out
        + jnp.einsum(
            "sqhk,skc->sqhc", weights[..., CACHE:], latent_slots, preferred_element_type=jnp.float32
        )
    ).astype(jnp.bfloat16)
    head_out = jnp.einsum(
        "sqhc,chv->sqhv",
        latent_out,
        value_up.reshape(KVRANK, heads_here, VDIM),
        preferred_element_type=jnp.float32,
    ).astype(jnp.bfloat16)
    request_out = jnp.dot(
        selector, head_out.reshape(seq_count, -1), preferred_element_type=jnp.float32
    )
    request_out = request_out.astype(jnp.bfloat16).reshape(seq_count * NEWTOK, heads_here * VDIM)
    out_rows = lax.all_to_all(out_cast, "tp", split_axis=0, concat_axis=1, tiled=True)
    partial_out = jnp.dot(
        request_out,
        lax.all_gather(out_rows, "dp", axis=1, tiled=True),
        preferred_element_type=jnp.float32,
    )
    reduced = lax.psum_scatter(partial_out, "tp", scatter_dimension=1, tiled=True)
    attention_out = reduced.astype(jnp.bfloat16).reshape(seq_count, NEWTOK, -1)
    return (attention_out, weight_norm)


def solution(mesh):
    in_specs = (
        P("dp", None, None),
        P("dp", None, None),
        P("dp", None, None),
        P("dp", None, None),
        P("dp", None, None),
        P("dp"),
        P("dp", None),
        P(("dp", "tp"), None),
        P(("dp", "tp"), None),
        P(("dp", "tp"), None),
        P(None, ("dp", "tp")),
    )
    out_specs = (P("dp", None, "tp"), P())
    return jax.shard_map(shards, mesh=mesh, in_specs=in_specs, out_specs=out_specs, check_vma=False)
```

profile of v0, /device:TPU:2, one launch (start us, length us, event | category | flops | bytes accessed | tf_op | source)
XLA Modules:
  0.0 952.9 jit_solution(7704429652962988391)
XLA Ops:
  7.2 2.6 multiply_reduce_fusion.3
  9.9 2.6 multiply_reduce_fusion.2
  12.5 4.5 multiply_reduce_fusion.1
  17.1 8.0 multiply_reduce_fusion
  25.2 0.4 copy.130
  25.6 44.1 %all_to_all.64 = bf16[4,2048,224]{1,2,0:T(8,128)(2,1)} all-to-all(bf16[4,2048,224]{1,2,0:T(8,128)(2,1)S(1)} %bitcast.89), channel_id=1, replica_groups=mesh['dp'=8,'tp'=4] {'tp'}, dimensions={0} | all-to-all | bytes 7340032 | tf_op jit(solution)/shard_map/all_to_all | solution.py:145
  69.7 14.5 %copy.71 = bf16[8,16,8192]{1,0,2:T(8,128)(2,1)} copy(bf16[8,16,8192]{2,1,0:T(8,128)(2,1)} %bitcast.100) | data formatting | bytes 4194304 | tf_op jit(solution)/shard_map/all_gather | solution.py:63
  84.2 20.3 %reshape.140 = bf16[4,2,131072]{2,1,0:T(2,128)(2,1)} reshape(bf16[8192,8,16]{2,1,0:T(8,128)(2,1)} %bitcast.83) | data formatting | bytes 4194304
  104.5 5.3 all-to-all-start.1
  109.9 0.4 all-gather.14.cloned.1.call-done
  110.3 14.5 %copy.82 = bf16[8,16,8192]{1,0,2:T(8,128)(2,1)} copy(bf16[8,16,8192]{2,1,0:T(8,128)(2,1)} %bitcast.101) | data formatting | bytes 4194304 | tf_op jit(solution)/shard_map/all_gather | solution.py:64
  124.7 20.3 %reshape.136 = bf16[4,2,131072]{2,1,0:T(2,128)(2,1)} reshape(bf16[8192,8,16]{2,1,0:T(8,128)(2,1)} %bitcast.84) | data formatting | bytes 4194304
  145.1 5.0 all-to-all-start.2
  150.0 98.8 %all-gather.10.cloned.1.call-done = bf16[384,12288]{1,0:T(8,128)(2,1)} async-done(((bf16[48,12288]{1,0:T(8,128)(2,1)}), bf16[384,12288]{1,0:T(8,128)(2,1)}) %all-gather.10.cloned.1.call-update) | async-done | bytes 9437200 | tf_op jit(solution)/shard_map/all_gather | solution.py:62
  248.8 26.0 %copy.67 = bf16[8,48,12288]{1,0,2:T(8,128)(2,1)} copy(bf16[8,48,12288]{2,1,0:T(8,128)(2,1)} %bitcast.92) | data formatting | bytes 18874368 | tf_op jit(solution)/shard_map/all_gather | solution.py:62
  274.9 54.9 %reshape.138 = bf16[4,2,589824]{2,1,0:T(2,128)(2,1)} reshape(bf16[12288,8,48]{2,1,0:T(8,128)(2,1)} %bitcast.81) | data formatting | bytes 18874368
  329.8 6.5 all-to-all-start
  336.2 1.8 copy.109
  338.0 1.8 convolution_convert_fusion.1
  339.9 4.1 reshape_reshape.9
  344.1 0.4 convolution_convert_fusion.3
  344.5 1.2 reshape.132
  345.6 0.3 convolution_convert_fusion.4
  345.9 0.1 copy.77
  346.0 0.8 copy.94
  347.0 2.9 multiply_cosine_fusion
  349.9 13.4 %reshape.141 = bf16[8192,8,16]{2,1,0:T(8,128)(2,1)} reshape(bf16[4,2,131072]{2,1,0:T(2,128)(2,1)S(1)} %all-to-all-done.1) | data formatting | bytes 4194304
  363.4 17.4 %copy.99 = bf16[8,16,4,2048]{3,2,1,0:T(4,128)(2,1)S(1)} copy(bf16[8,16,4,2048]{1,0,3,2:T(8,128)(2,1)} %bitcast.85) | data formatting | bytes 4194304 | tf_op jit(solution)/shard_map/all_to_all | solution.py:68
  380.8 1.2 copy.73
  381.9 2.1 copy.110
  384.0 14.3 %reshape.137 = bf16[8192,8,16]{2,1,0:T(8,128)(2,1)} reshape(bf16[4,2,131072]{2,1,0:T(2,128)(2,1)} %all-to-all-done.2) | data formatting | bytes 4194304
  398.4 17.4 %copy.104 = bf16[8,16,4,2048]{3,2,1,0:T(4,128)(2,1)S(1)} copy(bf16[8,16,4,2048]{1,0,3,2:T(8,128)(2,1)} %bitcast.86) | data formatting | bytes 4194304 | tf_op jit(solution)/shard_map/all_to_all | solution.py:69
  415.8 1.2 copy.84
  417.0 2.0 copy.112
  418.9 20.1 %all-to-all-done = bf16[4,2,589824]{2,1,0:T(2,128)(2,1)} async-done(((bf16[4,2,589824]{2,1,0:T(2,128)(2,1)}), bf16[4,2,589824]{2,1,0:T(2,128)(2,1)}, u32[]{:S(2)}, u32[]{:S(2)}) %all-to-all-start) | async-done | bytes 9437216 | tf_op jit(solution)/shard_map/all_to_all | solution.py:67
  439.0 40.7 %reshape.139 = bf16[12288,8,48]{2,1,0:T(8,128)(2,1)} reshape(bf16[4,2,589824]{2,1,0:T(2,128)(2,1)} %all-to-all-done) | data formatting | bytes 18874368
  479.8 28.1 %copy.98 = bf16[8,48,4,3072]{3,2,1,0:T(4,128)(2,1)} copy(bf16[8,48,4,3072]{1,0,3,2:T(8,128)(2,1)} %bitcast.82) | data formatting | bytes 18874368 | tf_op jit(solution)/shard_map/all_to_all | solution.py:67
  507.8 10.7 %copy.69 = bf16[8,4,48,3072]{3,2,1,0:T(8,128)(2,1)} copy(bf16[8,4,48,3072]{3,1,2,0:T(4,128)(2,1)} %bitcast.87) | data formatting | bytes 18874368 | tf_op jit(solution)/shard_map/all_to_all | solution.py:67
  518.5 8.1 convolution_convert_fusion.2
  526.6 5.6 reshape.117
  532.2 1.6 slice-done.1
  533.8 0.5 convert_element_type.66
  534.3 0.4 copy-done.8
  534.7 2.0 subtract_convert_fusion
  536.7 0.2 copy-done.5
  537.0 4.8 convert_bitcast_fusion
  541.8 4.8 fusion.8
  546.6 4.0 fusion.35
  550.6 23.9 %fusion.2 = f32[128,4,16,256]{3,2,1,0:T(8,128)} fusion(bf16[128,256,512]{2,1,0:T(8,128)(2,1)} %param.14, bf16[128,4,16,512]{3,0,1,2:T(8,128)(2,1)} %copy-done.3), kind=kOutput, calls=%fused_computation.2 | convolution fusion | flops 2147483648 | bytes 50331648 | tf_op jit(solution)/shard_map/sqhc,stc->sqht/dot_general | solution.py:104
  574.5 8.8 fusion.34
  583.4 3.6 fusion.5
  587.0 5.2 divide_convert_fusion
  592.2 21.1 %fusion = f32[128,4,16,512]{3,2,1,0:T(8,128)} fusion(bf16[128,256,512]{2,1,0:T(8,128)(2,1)} %param.14, bf16[128,4,16,260]{3,2,1,0:T(8,128)(2,1)} %divide_convert_fusion), kind=kOutput, calls=%fused_computation | convolution fusion | flops 2147483648 | bytes 54525952 | tf_op jit(solution)/shard_map/sqht,stc->sqhc/dot_general | solution.py:126
  613.4 10.4 %add_convert_fusion = bf16[128,4,16,512]{3,2,1,0:T(8,128)(2,1)} fusion(f32[128,4,16,512]{3,2,1,0:T(8,128)} %fusion, bf16[128,4,16,260]{3,2,1,0:T(8,128)(2,1)} %divide_convert_fusion, bf16[128,4,512,1]{2,1,0,3:T(4,128)(2,1)S(1)} %copy-done.6), kind=kOutput, calls=%fused_computation.4 | convolution fusion | flops 41943040 | bytes 27787264 | tf_op jit(solution)/shard_map/sqhk,skc->sqhc/dot_general | solution.py:131
  623.8 13.7 %convert_bitcast_fusion.1 = bf16[128,4,16,128]{0,3,1,2:T(8,128)(2,1)S(1)} fusion(bf16[512,16,128,1]{2,1,0,3:T(8,128)(2,1)S(1)} %bitcast.102, bf16[128,4,16,512]{3,2,1,0:T(8,128)(2,1)} %add_convert_fusion), kind=kOutput, calls=%fused_computation.34 | convolution fusion | flops 1074790400 | bytes 12582912 | tf_op jit(solution)/shard_map/sqhc,chv->sqhv/dot_general | solution.py:135
  637.5 0.1 copy.87
  637.6 0.8 convolution_convert_fusion
  638.4 2.8 reshape.123
  641.2 166.2 %all-gather.8.cloned.1.call-done = bf16[2048,7168]{0,1:T(8,128)(2,1)} async-done(((bf16[2048,896]{0,1:T(8,128)(2,1)}), bf16[2048,7168]{0,1:T(8,128)(2,1)}) %all-gather.8.cloned.1.call-update) | async-done | bytes 29360144 | tf_op jit(solution)/shard_map/all_gather | solution.py:148
  807.5 23.8 %fusion.36 = f32[512,7168]{1,0:T(8,128)} fusion(bf16[512,2048]{1,0:T(8,128)(2,1)} %reshape.123, bf16[2048,7168]{0,1:T(8,128)(2,1)} %all-gather.8.cloned.1.call-done), kind=kOutput, calls=%fused_computation.56 | convolution fusion | flops 15032385536 | bytes 46137344 | tf_op jit(solution)/shard_map/dot_general | solution.py:146
  833.8 40.9 %psum.7 = f32[]{:T(128)} all-reduce(f32[]{:T(128)S(6)} %add.51), channel_id=1, replica_groups=mesh['dp'=8,'tp'=4] {'dp','tp'}, use_global_device_ids=true, to_apply=%region_8.9 | all-reduce | flops 1 | bytes 8 | tf_op jit(solution)/shard_map/psum | solution.py:54
  875.4 65.7 %reduce-scatter.2.cloned.1.call-done = f32[512,1792]{1,0:T(8,128)} async-done(((f32[512,7168]{1,0:T(8,128)}), f32[512,1792]{1,0:T(8,128)}) %reduce-scatter.2.cloned.1.call-update) | async-done | bytes 3670032 | tf_op jit(solution)/shard_map/reduce_scatter | solution.py:151
  941.1 2.2 convert_element_type.77
  943.3 1.5 reshape.124
  (46 shorter events, 0.7 us)
Async XLA Ops:
  7.2 338.5 %copy-start = (bf16[128,4,64]{0,2,1:T(8,128)(2,1)S(1)}, bf16[128,4,64]{0,2,1:T(8,128)(2,1)}, u32[]{:S(2)}) copy-start(bf16[128,4,64]{0,2,1:T(8,128)(2,1)} %param.13) | copy-start | bytes 196612
  7.2 62.6 %all-gather.12.cloned.1.call-start = ((), (), s32[]{:S(2)}) async-start(), calls=%async_computation.8 | async-start | bytes 2359296 | tf_op jit(solution)/shard_map/all_gather | solution.py:63
  9.8 100.5 %all-gather.14.cloned.1.call-start = ((), (), s32[]{:S(2)}) async-start(), calls=%async_computation.9 | async-start | bytes 2359296 | tf_op jit(solution)/shard_map/all_gather | solution.py:64
  12.5 236.4 %all-gather.10.cloned.1.call-start = ((), (), s32[]{:S(2)}) async-start(), calls=%async_computation.7 | async-start | bytes 10616832 | tf_op jit(solution)/shard_map/all_gather | solution.py:62
  17.1 790.4 %all-gather.8.cloned.1.call-start = ((), (), s32[]{:S(2)}) async-start(), calls=%async_computation.5 | async-start | bytes 33030144 | tf_op jit(solution)/shard_map/all_gather | solution.py:148
  104.5 40.5 %all-to-all-start.1 = ((bf16[4,2,131072]{2,1,0:T(2,128)(2,1)}), bf16[4,2,131072]{2,1,0:T(2,128)(2,1)S(1)}, u32[]{:S(2)}, u32[]{:S(2)}) async-start(bf16[4,2,131072]{2,1,0:T(2,128)(2,1)} %reshape.140), calls=%async_computation.1 | async-start | bytes 4194304 | tf_op jit(solution)/shard_map/all_to_all | solution.py:68
  145.1 184.7 %all-to-all-start.2 = ((bf16[4,2,131072]{2,1,0:T(2,128)(2,1)}), bf16[4,2,131072]{2,1,0:T(2,128)(2,1)}, u32[]{:S(2)}, u32[]{:S(2)}) async-start(bf16[4,2,131072]{2,1,0:T(2,128)(2,1)} %reshape.136), calls=%async_computation.2 | async-start | bytes 4194304 | tf_op jit(solution)/shard_map/all_to_all | solution.py:69
  329.8 8.3 copy-start.11
  329.8 109.3 %all-to-all-start = ((bf16[4,2,589824]{2,1,0:T(2,128)(2,1)}), bf16[4,2,589824]{2,1,0:T(2,128)(2,1)}, u32[]{:S(2)}, u32[]{:S(2)}) async-start(bf16[4,2,589824]{2,1,0:T(2,128)(2,1)} %reshape.138), calls=%async_computation | async-start | bytes 18874368 | tf_op jit(solution)/shard_map/all_to_all | solution.py:67
  336.2 604.8 %reduce-scatter.2.cloned.1.call-start = ((), (), s32[]{:S(2)}) async-start(), calls=%async_computation.6 | async-start | bytes 18350080 | tf_op jit(solution)/shard_map/reduce_scatter | solution.py:151
  336.2 7.7 copy-start.10
  338.0 8.8 copy-start.12
  532.2 1.6 slice-start.1
  533.8 0.9 copy-start.8
  534.7 2.0 slice-start
  534.7 2.2 copy-start.5
  536.7 9.9 %copy-start.4 = (bf16[128,4,16,32]{3,2,1,0:T(8,128)(2,1)}, bf16[128,4,16,32]{3,2,1,0:T(8,128)(2,1)S(1)}, u32[]{:S(2)}) copy-start(bf16[128,4,16,32]{3,2,1,0:T(8,128)(2,1)S(1)} %get-tuple-element.5) | copy-start | bytes 1572868
  537.0 4.8 copy-start.6
  541.8 4.8 copy-start.3
  541.8 4.8 copy-start.9
  574.5 8.9 copy-start.2
  613.4 10.4 %copy-start.7 = (bf16[64,8,16,128]{3,2,1,0:T(8,128)(2,1)S(1)}, bf16[64,8,16,128]{3,2,1,0:T(8,128)(2,1)}, u32[]{:S(2)}) copy-start(bf16[64,8,16,128]{3,2,1,0:T(8,128)(2,1)} %copy.112) | copy-start | bytes 6291460
  875.4 69.4 %copy-start.1 = (bf16[128,4,64]{0,2,1:T(8,128)(2,1)S(1)}, bf16[128,4,64]{0,2,1:T(8,128)(2,1)}, u32[]{:S(2)}) copy-start(bf16[128,4,64]{0,2,1:T(8,128)(2,1)} %param.13) | copy-start | bytes 196612
Sparse Core Ops, SparseCore 0:
  10.1 50.2 all-gather.11
  62.6 47.6 all-gather.13
  113.0 135.7 all-gather.9
  250.2 557.1 all-gather.7
  831.4 109.6 reduce-scatter.1
where the time goes:
time: 965 us; the launch traced here: 953 us
  waiting for transfers between devices  351 us (36%)
  local copies, waits for them, and re-layouts  320 us (33%)
  matrix products  127 us (13%)
  blocking collectives  85 us (9%)
  other arithmetic  34.3 us (4%)
  between operations  18.9 us (2%)
  starting transfers between devices  17 us (2%)
    unnamed x36, local copies, waits for them, and re-layouts  171 us
    all_gather x1, waiting for transfers between devices, shards(): lax.all_gather(out_rows, 'dp', axis=1, tiled=True)  166 us
    all_gather x1, waiting for transfers between devices, shards(): lax.all_gather(query_cast[None], 'dp', axis=0, tiled=True)  98.8 us
    reduce_scatter x1, waiting for transfers between devices, shards(): lax.psum_scatter(partial_out, 'tp', scatter_dimension=1, tiled=True)  65.7 us
    all_to_all x1, blocking collectives, shards(): lax.all_to_all(out_cast, 'tp', split_axis=0, concat_axis=1, tiled=True)  44.1 us
    psum x1, blocking collectives, shards(): squares_total = lax.psum(local_squares, ('dp', 'tp'))  40.9 us
    all_to_all x2, local copies, waits for them, and re-layouts, shards(): lax.all_to_all(gathered[0], 'tp', split_axis=2, concat_axis=1, tiled=True)  38.7 us
    all_gather x1, local copies, waits for them, and re-layouts, shards(): lax.all_gather(query_cast[None], 'dp', axis=0, tiled=True)  26 us
  transfers between devices with their start and end apart: 8, of which 5 were waited for; matrix products, arithmetic and copies ran while one was open for 47% of the time, Pallas kernels for 0%

commit v1 on v0

--- a/solution.py
+++ b/solution.py
@@ -58,19 +58,13 @@
     query_cast = w_uq.astype(jnp.bfloat16)
     key_cast = w_uk.astype(jnp.bfloat16)
     value_cast = w_uv.astype(jnp.bfloat16)
-    gathered = (
-        lax.all_gather(query_cast[None], "dp", axis=0, tiled=True),
-        lax.all_gather(key_cast[None], "dp", axis=0, tiled=True),
-        lax.all_gather(value_cast[None], "dp", axis=0, tiled=True),
-    )
-    mixed = (
-        lax.all_to_all(gathered[0], "tp", split_axis=2, concat_axis=1, tiled=True),
-        lax.all_to_all(gathered[1], "tp", split_axis=2, concat_axis=1, tiled=True),
-        lax.all_to_all(gathered[2], "tp", split_axis=2, concat_axis=1, tiled=True),
-    )
-    query_up = mixed[0].reshape(-1, mixed[0].shape[2])
-    key_up = mixed[1].reshape(-1, mixed[1].shape[2])
-    value_up = mixed[2].reshape(-1, mixed[2].shape[2])
+    def regroup(block):
+        mixed = lax.all_to_all(block, "tp", split_axis=1, concat_axis=0, tiled=True)
+        return lax.all_gather(mixed, "dp", axis=0, tiled=True)
+
+    query_up = regroup(query_cast)
+    key_up = regroup(key_cast)
+    value_up = regroup(value_cast)
     out_cast = w_o.astype(jnp.bfloat16)
     seq_count = q_latent.shape[0]
     heads_here = key_up.shape[1] // NOPE
@@ -142,14 +136,29 @@
         selector, head_out.reshape(seq_count, -1), preferred_element_type=jnp.float32
     )
     request_out = request_out.astype(jnp.bfloat16).reshape(seq_count * NEWTOK, heads_here * VDIM)
+    tp = lax.axis_size("tp")
+    dp = lax.axis_size("dp")
+    near = dp // tp
     out_rows = lax.all_to_all(out_cast, "tp", split_axis=0, concat_axis=1, tiled=True)
-    partial_out = jnp.dot(
-        request_out,
-        lax.all_gather(out_rows, "dp", axis=1, tiled=True),
-        preferred_element_type=jnp.float32,
+    near_groups = [[i * near + j for j in range(near)] for i in range(tp)]
+    far_groups = [[i * near + j for i in range(tp)] for j in range(near)]
+    out_block = lax.all_gather(
+        out_rows, "dp", axis=1, tiled=True, axis_index_groups=near_groups
     )
-    reduced = lax.psum_scatter(partial_out, "tp", scatter_dimension=1, tiled=True)
-    attention_out = reduced.astype(jnp.bfloat16).reshape(seq_count, NEWTOK, -1)
+    all_heads = lax.all_gather(
+        request_out, "dp", axis=0, tiled=True, axis_index_groups=far_groups
+    )
+    partial_out = jnp.dot(all_heads, out_block, preferred_element_type=jnp.float32)
+    reduced = lax.psum_scatter(
+        partial_out.astype(jnp.bfloat16), "tp", scatter_dimension=0, tiled=True
+    )
+    pairs = []
+    for i in range(tp):
+        for j in range(near):
+            for t in range(tp):
+                pairs.append(((i * near + j) * tp + t, (t * near + j) * tp + i))
+    moved = lax.ppermute(reduced, ("dp", "tp"), pairs)
+    attention_out = moved.reshape(seq_count, NEWTOK, -1)
     return (attention_out, weight_norm)
 
 

time: 965 us -> 748 us (0.78)
  local copies, waits for them, and re-layouts: 320 us -> 30 us
  blocking collectives: 85 us -> 135 us
  waiting for transfers between devices: 351 us -> 387 us
    unnamed x36 -> x22, local copies, waits for them, and re-layouts: 171 us -> 3.68 us
    all_to_all x6 -> x3, local copies, waits for them, and re-layouts: 75.9 us -> 0.12 us  [regroup(): mixed = lax.all_to_all(block, 'tp', split_axis=1, concat_axis=0, tiled=True)]
    psum x1, blocking collectives: 40.9 us -> 99.3 us  [shards(): squares_total = lax.psum(local_squares, ('dp', 'tp'))]
    all_gather x3 -> x2, local copies, waits for them, and re-layouts: 55 us -> 6.79 us  [regroup(): return lax.all_gather(mixed, 'dp', axis=0, tiled=True)]
    all_gather x4 -> x5, waiting for transfers between devices: 265 us -> 291 us  [the longest x1 148 us: shards(): lax.all_gather(request_out, 'dp', axis=0, tiled=True, axis_index_groups=f...]
    all_to_all x3 -> x1, waiting for transfers between devices: 20.1 us -> 33.5 us  [shards(): lax.all_to_all(out_cast, 'tp', split_axis=0, concat_axis=1, tiled=True)]
    all_to_all x3 -> x1, starting transfers between devices: 16.8 us -> 6.45 us  [shards(): lax.all_to_all(out_cast, 'tp', split_axis=0, concat_axis=1, tiled=True)]
    all_to_all x1 -> x3, blocking collectives: 44.1 us -> 35.6 us  [regroup(): mixed = lax.all_to_all(block, 'tp', split_axis=1, concat_axis=0, tiled=True)]
  transfers between devices with their start and end apart: 8 -> 8, of which waited for: 5 -> 5; matrix products, arithmetic and copies ran while one was open for 47% -> 21% of each run, Pallas kernels for 0% -> 0%
where the time goes in v1:
time: 748 us; the launch traced here: 739 us
  waiting for transfers between devices  387 us (52%)
  blocking collectives  135 us (18%)
  matrix products  122 us (16%)
  other arithmetic  34.2 us (5%)
  local copies, waits for them, and re-layouts  30 us (4%)
  between operations  19 us (3%)
  starting transfers between devices  12.1 us (2%)
    all_gather x1, waiting for transfers between devices, shards(): lax.all_gather(request_out, 'dp', axis=0, tiled=True, axis_index_groups=f...  148 us
    all_gather x3, waiting for transfers between devices, regroup(): return lax.all_gather(mixed, 'dp', axis=0, tiled=True)  143 us
    psum x1, blocking collectives, shards(): squares_total = lax.psum(local_squares, ('dp', 'tp'))  99.3 us
    reduce_scatter x1, waiting for transfers between devices, shards(): lax.psum_scatter(partial_out.astype(jnp.bfloat16), 'tp', scatter_dimensio...  63.2 us
    all_to_all x3, blocking collectives, regroup(): mixed = lax.all_to_all(block, 'tp', split_axis=1, concat_axis=0, tiled=True)  35.6 us
    all_to_all x1, waiting for transfers between devices, shards(): lax.all_to_all(out_cast, 'tp', split_axis=0, concat_axis=1, tiled=True)  33.5 us
    dot_general x1, matrix products, shards(): jnp.einsum('sqhc,stc->sqht', absorbed, cache_latent, preferred_element_ty...  23.3 us
    dot_general x1, matrix products, shards(): jnp.dot(all_heads, out_block, preferred_element_type=jnp.float32)  21.4 us
  transfers between devices with their start and end apart: 8, of which 5 were waited for; matrix products, arithmetic and copies ran while one was open for 21% of the time, Pallas kernels for 0%

profile of v1, /device:TPU:2, one launch (start us, length us, event | category | flops | bytes accessed | tf_op | source)
XLA Modules:
  0.0 739.3 jit_solution(5233943075332913115)
XLA Ops:
  7.2 0.0 all-gather.8.cloned.1.call-start
  7.2 2.2 multiply_reduce_fusion.3
  9.4 7.6 %all_to_all.76 = bf16[16,4,2048]{2,0,1:T(8,128)(2,1)} all-to-all(bf16[16,4,2048]{2,0,1:T(8,128)(2,1)S(1)} %bitcast.99), channel_id=1, replica_groups=mesh['dp'=8,'tp'=4] {'tp'}, dimensions={1} | all-to-all | bytes 524288 | tf_op jit(solution)/shard_map/all_to_all | solution.py:62
  17.0 0.0 all-gather.8.cloned.1.call-update
  17.0 0.0 all-gather.10.cloned.1.call-start
  17.1 2.1 multiply_reduce_fusion.2
  19.2 9.1 %all_to_all.77 = bf16[16,4,2048]{2,0,1:T(8,128)(2,1)} all-to-all(bf16[16,4,2048]{2,0,1:T(8,128)(2,1)S(1)} %bitcast.100), channel_id=1, replica_groups=mesh['dp'=8,'tp'=4] {'tp'}, dimensions={1} | all-to-all | bytes 524288 | tf_op jit(solution)/shard_map/all_to_all | solution.py:62
  28.2 0.0 all-gather.10.cloned.1.call-update
  28.2 0.0 all-gather.6.cloned.1.call-start
  28.3 1.2 multiply_reduce_fusion.1
  29.5 0.1 copy.99
  29.6 19.0 %all_to_all.78 = bf16[48,4,3072]{2,0,1:T(8,128)(2,1)} all-to-all(bf16[48,4,3072]{2,0,1:T(8,128)(2,1)S(1)} %bitcast.92), channel_id=1, replica_groups=mesh['dp'=8,'tp'=4] {'tp'}, dimensions={1} | all-to-all | bytes 2359296 | tf_op jit(solution)/shard_map/all_to_all | solution.py:62
  48.6 0.0 all-gather.6.cloned.1.call-update
  48.6 7.8 %multiply_reduce_fusion = (f32[]{:T(128)}, bf16[8192,224]{0,1:T(8,128)(2,1)S(1)}) fusion(f32[8192,224]{0,1:T(8,128)} %param.21), kind=kLoop, calls=%fused_computation.18 | loop fusion | flops 5505023 | bytes 11010052 | tf_op jit(solution)/shard_map/reduce_sum | solution.py:52
  56.4 2.4 copy.98
  58.8 6.5 all-to-all-start.3
  65.3 0.3 copy.82
  65.6 0.7 convolution_convert_fusion.2
  66.3 2.0 reshape_reshape.3
  68.3 0.1 copy.83
  68.4 0.4 convolution_convert_fusion.4
  68.8 0.4 reshape.139
  69.2 0.3 convolution_convert_fusion.5
  69.4 0.1 copy.54
  69.6 0.1 copy.69
  69.7 0.1 iota_compare_fusion
  69.8 0.1 add_convert_fusion.2
  69.9 2.9 multiply_cosine_fusion
  72.8 33.5 %all-to-all-done.3 = bf16[4,2048,224]{1,2,0:T(8,128)(2,1)} async-done(((bf16[4,2048,224]{1,2,0:T(8,128)(2,1)}), bf16[4,2048,224]{1,2,0:T(8,128)(2,1)}, u32[]{:S(2)}, u32[]{:S(2)}) %all-to-all-start.3) | async-done | bytes 3670048 | tf_op jit(solution)/shard_map/all_to_all | solution.py:142
  106.3 0.0 all-gather.14.cloned.1.call-update
  106.3 0.0 all-gather.12.cloned.1.call-start
  106.3 0.0 all-gather.8.cloned.1.call-done
  106.4 2.9 copy.50
  109.2 8.6 %all-gather.10.cloned.1.call-done = bf16[512,2048]{1,0:T(8,128)(2,1)} async-done(((bf16[64,2048]{1,0:T(8,128)(2,1)}), bf16[512,2048]{1,0:T(8,128)(2,1)}) %all-gather.10.cloned.1.call-update) | async-done | bytes 2097168 | tf_op jit(solution)/shard_map/all_gather | solution.py:63
  117.8 3.9 copy.60
  121.8 134.1 %all-gather.6.cloned.1.call-done = bf16[1536,3072]{1,0:T(8,128)(2,1)} async-done(((bf16[192,3072]{1,0:T(8,128)(2,1)}), bf16[1536,3072]{1,0:T(8,128)(2,1)}) %all-gather.6.cloned.1.call-update) | async-done | bytes 9437200 | tf_op jit(solution)/shard_map/all_gather | solution.py:63
  255.8 9.2 %convolution_convert_fusion.3 = bf16[512,3072]{1,0:T(8,128)(2,1)} fusion(bf16[512,1536]{1,0:T(8,128)(2,1)} %reshape_reshape.3, bf16[1536,3072]{1,0:T(8,128)(2,1)} %all-gather.6.cloned.1.call-done), kind=kOutput, calls=%fused_computation.20 | convolution fusion | flops 4833411072 | bytes 14155776 | tf_op jit(solution)/shard_map/dot_general | solution.py:84
  265.1 8.4 %reshape.125 = bf16[128,4,16,192]{3,2,1,0:T(8,128)(2,1)} reshape(bf16[512,3072]{1,0:T(8,128)(2,1)} %convolution_convert_fusion.3) | data formatting | bytes 6291456 | tf_op jit(solution)/shard_map/reshape | solution.py:87
  273.4 1.6 slice-done.1
  275.0 2.4 convert_element_type.66
  277.5 4.0 convert_bitcast_fusion
  281.5 3.2 copy-done.2
  284.8 6.8 fusion.8
  291.5 23.3 %fusion.2 = f32[128,4,16,256]{3,2,1,0:T(8,128)} fusion(bf16[128,256,512]{2,1,0:T(8,128)(2,1)} %param.14, bf16[128,4,16,512]{3,0,1,2:T(8,128)(2,1)} %copy-done.2), kind=kOutput, calls=%fused_computation.2 | convolution fusion | flops 2147483648 | bytes 50331648 | tf_op jit(solution)/shard_map/sqhc,stc->sqht/dot_general | solution.py:98
  314.9 5.2 subtract_convert_fusion
  320.0 3.5 fusion.31
  323.5 7.3 fusion.30
  330.8 1.0 reduce_max.22
  331.9 3.6 fusion.5
  335.5 5.7 divide_convert_fusion
  341.1 21.1 %fusion = f32[128,4,16,512]{3,2,1,0:T(8,128)} fusion(bf16[128,256,512]{2,1,0:T(8,128)(2,1)} %param.14, bf16[128,4,16,260]{3,2,1,0:T(8,128)(2,1)} %divide_convert_fusion), kind=kOutput, calls=%fused_computation | convolution fusion | flops 2147483648 | bytes 54525952 | tf_op jit(solution)/shard_map/sqht,stc->sqhc/dot_general | solution.py:120
  362.2 10.2 %add_convert_fusion = bf16[128,4,16,512]{3,2,1,0:T(8,128)(2,1)} fusion(f32[128,4,16,512]{3,2,1,0:T(8,128)} %fusion, bf16[128,4,16,260]{3,2,1,0:T(8,128)(2,1)} %divide_convert_fusion, bf16[128,4,512,1]{2,1,0,3:T(4,128)(2,1)S(1)} %reshape.139), kind=kOutput, calls=%fused_computation.4 | convolution fusion | flops 41943040 | bytes 27787264 | tf_op jit(solution)/shard_map/sqhk,skc->sqhc/dot_general | solution.py:125
  372.4 12.6 %convert_bitcast_fusion.1 = bf16[128,4,16,128]{0,3,1,2:T(8,128)(2,1)S(1)} fusion(bf16[512,16,128,1]{0,2,3,1:T(8,128)(2,1)S(1)} %bitcast.94, bf16[128,4,16,512]{3,2,1,0:T(8,128)(2,1)} %add_convert_fusion), kind=kOutput, calls=%fused_computation.33 | convolution fusion | flops 1074790400 | bytes 12582912 | tf_op jit(solution)/shard_map/sqhc,chv->sqhv/dot_general | solution.py:129
  385.0 0.1 copy.62
  385.2 0.8 convolution_convert_fusion
  385.9 2.9 reshape.133
  388.9 0.0 reduce-scatter.2.cloned.1.call-start
  388.9 0.0 all-gather.14.cloned.1.call-done
  388.9 148.1 %all-gather.12.cloned.1.call-done = bf16[2048,2048]{1,0:T(8,128)(2,1)} async-done(((bf16[512,2048]{1,0:T(8,128)(2,1)}), bf16[2048,2048]{1,0:T(8,128)(2,1)}) %all-gather.12.cloned.1.call-update) | async-done | bytes 8388624 | tf_op jit(solution)/shard_map/all_gather | solution.py:148
  537.0 21.4 %convolution_convert_fusion.1 = bf16[2048,1792]{1,0:T(8,128)(2,1)} fusion(bf16[2048,2048]{1,0:T(8,128)(2,1)} %all-gather.12.cloned.1.call-done, bf16[2048,1792]{0,1:T(8,128)(2,1)} %all-gather.14.cloned.1.call-done), kind=kOutput, calls=%fused_computation.14 | convolution fusion | flops 15036055552 | bytes 23068672 | tf_op jit(solution)/shard_map/dot_general | solution.py:151
  558.4 63.2 %reduce-scatter.2.cloned.1.call-done = bf16[512,1792]{1,0:T(8,128)(2,1)} async-done(((bf16[2048,1792]{1,0:T(8,128)(2,1)}), bf16[512,1792]{1,0:T(8,128)(2,1)}) %reduce-scatter.2.cloned.1.call-update) | async-done | bytes 1835024 | tf_op jit(solution)/shard_map/reduce_scatter | solution.py:152
  621.6 5.4 collective-permute-start
  629.7 99.3 %psum.7 = f32[]{:T(128)} all-reduce(f32[]{:T(128)S(6)} %add.51), channel_id=1, replica_groups=mesh['dp'=8,'tp'=4] {'dp','tp'}, use_global_device_ids=true, to_apply=%region_8.9 | all-reduce | flops 1 | bytes 8 | tf_op jit(solution)/shard_map/psum | solution.py:54
  729.6 1.5 reshape.134
  (30 shorter events, 0.1 us)
Async XLA Ops:
  7.2 62.0 %copy-start = (bf16[128,4,64]{0,2,1:T(8,128)(2,1)S(1)}, bf16[128,4,64]{0,2,1:T(8,128)(2,1)}, u32[]{:S(2)}) copy-start(bf16[128,4,64]{0,2,1:T(8,128)(2,1)} %param.13) | copy-start | bytes 196612
  7.2 21.1 %copy-start.4 = (f32[48,12288]{1,0:T(8,128)S(1)}, f32[48,12288]{1,0:T(8,128)}, u32[]{:S(2)}) copy-start(f32[48,12288]{1,0:T(8,128)} %param.18) | copy-start | bytes 7077892
  7.2 99.2 %all-gather.8.cloned.1.call-start = ((), (), s32[]{:S(2)}) async-start(), calls=%async_computation.6 | async-start | bytes 2359296 | tf_op jit(solution)/shard_map/all_gather | solution.py:63
  17.0 100.8 %all-gather.10.cloned.1.call-start = ((), (), s32[]{:S(2)}) async-start(), calls=%async_computation.7 | async-start | bytes 2359296 | tf_op jit(solution)/shard_map/all_gather | solution.py:63
  28.2 227.6 %all-gather.6.cloned.1.call-start = ((), (), s32[]{:S(2)}) async-start(), calls=%async_computation.5 | async-start | bytes 10616832 | tf_op jit(solution)/shard_map/all_gather | solution.py:63
  58.8 6.5 copy-start.6
  58.8 6.8 copy-start.8
  58.8 47.4 %all-to-all-start.3 = ((bf16[4,2048,224]{1,2,0:T(8,128)(2,1)}), bf16[4,2048,224]{1,2,0:T(8,128)(2,1)}, u32[]{:S(2)}, u32[]{:S(2)}) async-start(bf16[4,2048,224]{1,2,0:T(8,128)(2,1)} %bitcast.86), calls=%async_computation.3 | async-start | bytes 7340032 | tf_op jit(solution)/shard_map/all_to_all | solution.py:142
  65.3 323.7 %all-gather.14.cloned.1.call-start = ((), (), s32[]{:S(2)}) async-start(), calls=%async_computation.9 | async-start | bytes 11010048 | tf_op jit(solution)/shard_map/all_gather | solution.py:145
  65.3 3.0 copy-start.7
  65.6 4.1 copy-start.9
  106.3 430.7 %all-gather.12.cloned.1.call-start = ((), (), s32[]{:S(2)}) async-start(), calls=%async_computation.8 | async-start | bytes 10485760 | tf_op jit(solution)/shard_map/all_gather | solution.py:148
  273.4 1.6 slice-start.1
  275.0 2.5 slice-start
  281.5 3.3 copy-start.2
  314.9 5.2 copy-start.3
  362.2 10.2 %copy-start.5 = (bf16[512,2048]{0,1:T(8,128)(2,1)S(1)}, bf16[512,2048]{0,1:T(8,128)(2,1)}, u32[]{:S(2)}) copy-start(bf16[512,2048]{0,1:T(8,128)(2,1)} %copy.60) | copy-start | bytes 6291460
  388.9 232.8 %reduce-scatter.2.cloned.1.call-start = ((), (), s32[]{:S(2)}) async-start(), calls=%async_computation.10 | async-start | bytes 9175040 | tf_op jit(solution)/shard_map/reduce_scatter | solution.py:152
  558.4 172.7 %copy-start.1 = (bf16[128,4,64]{0,2,1:T(8,128)(2,1)S(1)}, bf16[128,4,64]{0,2,1:T(8,128)(2,1)}, u32[]{:S(2)}) copy-start(bf16[128,4,64]{0,2,1:T(8,128)(2,1)} %param.13) | copy-start | bytes 196612
  621.6 108.0 %collective-permute-start = (bf16[512,1792]{1,0:T(8,128)(2,1)}, bf16[512,1792]{1,0:T(8,128)(2,1)S(1)}, u32[]{:S(2)}, u32[]{:S(2)}) collective-permute-start(bf16[512,1792]{1,0:T(8,128)(2,1)} %reduce-scatter.2.cloned.1.call-done), channel_id=1, source_target_pairs={{0,0},{1,8},{2,16},{3,24},{4,4},{5,12},{6,20},{7,28},{8,1},{9,9},{... | collective-permute-start | bytes 5505032 | tf_op jit(solution)/shard_map/ppermute | solution.py:160
Sparse Core Ops, SparseCore 0:
  17.1 50.8 all-gather.7
  70.2 47.6 all-gather.9
  120.0 135.7 all-gather.5
  257.2 90.3 all-gather.13
  389.0 147.9 all-gather.11
  558.6 63.0 reduce-scatter.1

commit v2 on v0

v2 whole, which is shorter than its diff:
```python
import functools

import jax
import jax.numpy as jnp
from jax import lax
from jax.experimental import pallas as pl
from jax.experimental.pallas import tpu as pltpu
from jax.sharding import PartitionSpec as P

D = 7168
QRANK = 1536
KVRANK = 512
NOPE = 128
ROPE = 64
VDIM = 128
HEADS = 64
NEWTOK = 4
CACHE = 256
CHUNKS = 2
GROUP = 4


def widen(values):
    return lax.optimization_barrier(values).astype(jnp.float32)


def rotate_half(values, positions):
    half_width = values.shape[-1] // 2
    frequency = 10000.0 ** (-jnp.arange(half_width, dtype=jnp.float32) / half_width)
    angles = positions.astype(jnp.float32)[:, :, None, None] * frequency
    cosine = jnp.cos(angles)
    sine_part = jnp.sin(angles)
    lower_half = values[..., :half_width]
    upper_half = values[..., half_width:]
    return jnp.concatenate(
        [
            lower_half * cosine - upper_half * sine_part,
            upper_half * cosine + lower_half * sine_part,
        ],
        axis=-1,
    )


def attention_kernel(
    heads, per_step, base, len_ref, query_ref, rot_ref, cache_ref, rope_ref, new_ref, new_rope_ref, out_ref
):
    scale = (NOPE + ROPE) ** (-0.5)
    rows = query_ref.shape[1]
    step = pl.program_id(0)
    slot = lax.broadcasted_iota(jnp.int32, (rows, CACHE), 1)
    token = lax.broadcasted_iota(jnp.int32, (rows, NEWTOK), 0) // heads
    other = lax.broadcasted_iota(jnp.int32, (rows, NEWTOK), 1)
    across = (((1,), (1,)), ((), ()))
    for group in range(0, per_step, GROUP):
        members = range(group, group + GROUP)
        raw = []
        for i in members:
            old_scores = lax.dot_general(
                query_ref[i], cache_ref[i], across, preferred_element_type=jnp.float32
            )
            old_scores += jnp.dot(rot_ref[i], rope_ref[i], preferred_element_type=jnp.float32)
            new_scores = lax.dot_general(
                query_ref[i], new_ref[i], across, preferred_element_type=jnp.float32
            )
            new_scores += lax.dot_general(
                rot_ref[i], new_rope_ref[i], across, preferred_element_type=jnp.float32
            )
            raw.append((old_scores, new_scores))
        weights = []
        for i, (old_scores, new_scores) in zip(members, raw):
            length = len_ref[base + step * per_step + i]
            old_scores = jnp.where(slot < length, old_scores * scale, -jnp.inf)
            new_scores = jnp.where(token >= other, new_scores * scale, -jnp.inf)
            largest = jnp.maximum(
                jnp.max(old_scores, axis=-1, keepdims=True),
                jnp.max(new_scores, axis=-1, keepdims=True),
            )
            old = jnp.exp(old_scores - largest)
            fresh = jnp.exp(new_scores - largest)
            total = jnp.sum(old, axis=-1, keepdims=True) + jnp.sum(fresh, axis=-1, keepdims=True)
            weights.append(
                ((old / total).astype(jnp.bfloat16), (fresh / total).astype(jnp.bfloat16))
            )
        mixed = []
        for i, (old, fresh) in zip(members, weights):
            result = jnp.dot(old, cache_ref[i], preferred_element_type=jnp.float32)
            result += jnp.dot(fresh, new_ref[i], preferred_element_type=jnp.float32)
            mixed.append(result.astype(jnp.bfloat16))
        for i, result in zip(members, mixed):
            out_ref[i] = result


def attend(heads, chunk, count, lengths, *arrays):
    per_step = 8
    first = chunk * count // per_step

    def spec(array):
        begin = 0 if array.shape[0] == count else first
        return pl.BlockSpec((per_step,) + array.shape[1:], lambda i: (begin + i, 0, 0))

    rows = arrays[0].shape[1]
    return pl.pallas_call(
        functools.partial(attention_kernel, heads, per_step, chunk * count),
        grid=(count // per_step,),
        out_shape=jax.ShapeDtypeStruct((count, rows, KVRANK), jnp.bfloat16),
        in_specs=[pl.BlockSpec(memory_space=pltpu.SMEM)] + [spec(array) for array in arrays],
        out_specs=pl.BlockSpec((per_step, rows, KVRANK), lambda i: (i, 0, 0)),
        compiler_params=pltpu.CompilerParams(vmem_limit_bytes=32 * 1024 * 1024),
        cost_estimate=pl.CostEstimate(
            flops=4 * count * rows * CACHE * KVRANK * 4,
            bytes_accessed=count * CACHE * KVRANK * 4,
            transcendentals=count * rows * CACHE,
        ),
        name="attend",
    )(lengths, *arrays)


def shards(
    q_latent,
    new_latent,
    new_rope,
    cache_latent,
    cache_rope,
    lengths,
    assignment,
    w_uq,
    w_uk,
    w_uv,
    w_o,
):
    local_squares = (
        jnp.sum(w_uq * w_uq) + jnp.sum(w_uk * w_uk) + jnp.sum(w_uv * w_uv) + jnp.sum(w_o * w_o)
    )
    squares_total = lax.psum(local_squares, ("dp", "tp"))
    tp = lax.axis_size("tp")
    dp = lax.axis_size("dp")
    near = dp // tp

    def swap(block):
        return lax.all_to_all(block, "tp", split_axis=1, concat_axis=0, tiled=True)

    def gather(block):
        return lax.all_gather(block, "dp", axis=0, tiled=True)

    query_mixed = swap(w_uq.astype(jnp.bfloat16))
    query_mixed, key_cast = lax.optimization_barrier((query_mixed, w_uk.astype(jnp.bfloat16)))
    key_mixed = swap(key_cast)
    key_mixed, value_cast, out_cast = lax.optimization_barrier(
        (key_mixed, w_uv.astype(jnp.bfloat16), w_o.astype(jnp.bfloat16))
    )
    value_mixed = swap(value_cast)
    query_up = gather(query_mixed)
    key_mixed, squares_total = lax.optimization_barrier((key_mixed, squares_total))
    query_up, key_mixed = lax.optimization_barrier((query_up, key_mixed))
    key_up = gather(key_mixed)
    out_rows = lax.all_to_all(out_cast, "tp", split_axis=0, concat_axis=1, tiled=True)
    key_up, value_mixed, out_rows = lax.optimization_barrier((key_up, value_mixed, out_rows))
    value_up = gather(value_mixed)
    width = out_rows.shape[1]
    place = lax.rem(lax.axis_index("dp"), near)
    out_block = lax.dynamic_update_slice(
        jnp.zeros((out_rows.shape[0], near * width), jnp.bfloat16), out_rows, (0, place * width)
    )
    for shift in range(1, near):
        pairs = [(d, d // near * near + (d + shift) % near) for d in range(dp)]
        arrived = lax.ppermute(out_rows, "dp", pairs)
        source = lax.rem(place + near - shift, near)
        out_block = lax.dynamic_update_slice(out_block, arrived, (0, source * width))
    seq_count = q_latent.shape[0]
    heads_here = key_up.shape[1] // NOPE
    selector = (assignment[0][:, None] == jnp.arange(seq_count, dtype=jnp.int32)[None, :]).astype(
        jnp.bfloat16
    )

    def to_slots(array):
        moved = jnp.dot(
            selector.T, array.reshape(seq_count, -1), preferred_element_type=jnp.float32
        )
        return moved.astype(jnp.bfloat16).reshape(array.shape)

    query_slots = to_slots(q_latent)
    latent_slots = to_slots(new_latent)
    rope_slots = to_slots(new_rope)
    weight_norm = jnp.sqrt(squares_total / (HEADS * (NOPE + ROPE) + 2 * HEADS * NOPE + D)).reshape(
        1
    )
    projected = jnp.dot(
        query_slots.reshape(seq_count * NEWTOK, QRANK), query_up, preferred_element_type=jnp.float32
    )
    projected = projected.astype(jnp.bfloat16).reshape(seq_count, NEWTOK, heads_here, NOPE + ROPE)
    query_nope = projected[..., :NOPE]
    positions = lengths[:, None] + jnp.arange(NEWTOK, dtype=jnp.int32)[None, :]
    query_rot = rotate_half(widen(projected[..., NOPE:]), positions).astype(jnp.bfloat16)
    ring = [(d, (d + near) % dp) for d in range(dp)]
    crossing = []
    for i in range(tp):
        for j in range(near):
            for t in range(tp):
                crossing.append(((i * near + j) * tp + t, (t * near + j) * tp + i))
    far = lax.axis_index("dp") // near
    value_heads = value_up.reshape(KVRANK, heads_here, VDIM)
    per_chunk = seq_count // CHUNKS
    key_heads = key_up.reshape(KVRANK, heads_here, NOPE)
    blocks = []
    for chunk in range(CHUNKS):
        rows = slice(chunk * per_chunk, (chunk + 1) * per_chunk)
        absorbed = jnp.einsum(
            "sqhn,chn->sqhc", query_nope[rows], key_heads, preferred_element_type=jnp.float32
        ).astype(jnp.bfloat16)
        latent_out = attend(
            heads_here,
            chunk,
            per_chunk,
            lengths,
            absorbed.reshape(per_chunk, NEWTOK * heads_here, KVRANK),
            query_rot[rows].reshape(per_chunk, NEWTOK * heads_here, ROPE),
            cache_latent,
            cache_rope,
            latent_slots,
            rope_slots,
        )
        head_out = jnp.einsum(
            "sqhc,chv->sqhv",
            latent_out.reshape(per_chunk, NEWTOK, heads_here, KVRANK),
            value_heads,
            preferred_element_type=jnp.float32,
        ).astype(jnp.bfloat16)
        blocks.append(head_out.reshape(per_chunk * NEWTOK, heads_here * VDIM))
    rows = per_chunk * NEWTOK
    partials = [jnp.zeros((tp * rows, near * width), jnp.bfloat16) for _ in blocks]
    arrived = [lax.ppermute(block, "dp", ring) for block in blocks]
    if CHUNKS > 1:
        arrived[0], blocks[-1] = lax.optimization_barrier((arrived[0], blocks[-1]))
    for step in range(tp):
        for chunk in range(CHUNKS):
            product = jnp.dot(blocks[chunk], out_block, preferred_element_type=jnp.float32)
            owner = lax.rem(far + tp - step, tp)
            partials[chunk] = lax.dynamic_update_slice(
                partials[chunk], product.astype(jnp.bfloat16), (owner * rows, 0)
            )
            if step < tp - 1:
                blocks[chunk] = arrived[chunk]
                if step < tp - 2:
                    arrived[chunk] = lax.ppermute(arrived[chunk], "dp", ring)
    pieces = []
    for partial_out in partials:
        reduced = lax.psum_scatter(partial_out, "tp", scatter_dimension=0, tiled=True)
        pieces.append(lax.ppermute(reduced, ("dp", "tp"), crossing))
    slot_out = jnp.concatenate(pieces, axis=0).reshape(seq_count, -1)
    attention_out = jnp.dot(selector, slot_out, preferred_element_type=jnp.float32)
    attention_out = attention_out.astype(jnp.bfloat16).reshape(seq_count, NEWTOK, -1)
    return (attention_out, weight_norm)


def solution(mesh):
    in_specs = (
        P("dp", None, None),
        P("dp", None, None),
        P("dp", None, None),
        P("dp", None, None),
        P("dp", None, None),
        P("dp"),
        P("dp", None),
        P(("dp", "tp"), None),
        P(("dp", "tp"), None),
        P(("dp", "tp"), None),
        P(None, ("dp", "tp")),
    )
    out_specs = (P("dp", None, "tp"), P())
    return jax.shard_map(shards, mesh=mesh, in_specs=in_specs, out_specs=out_specs, check_vma=False)
```

time: 965 us -> 573 us (0.59)
  local copies, waits for them, and re-layouts: 320 us -> 60.6 us
  matrix products: 127 us -> 58.5 us
  waiting for transfers between devices: 351 us -> 302 us
  blocking collectives: 85 us -> 44.7 us
  Pallas kernels: 0 us -> 31.6 us
  other arithmetic: 34.3 us -> 21.8 us
  starting transfers between devices: 17 us -> 27.5 us
    all_gather x4 -> x3, waiting for transfers between devices: 265 us -> 77.3 us  [gather(): return lax.all_gather(block, 'dp', axis=0, tiled=True)]
    unnamed x36 -> x46, local copies, waits for them, and re-layouts: 171 us -> 8.95 us
    ppermute x0 -> x9, waiting for transfers between devices: none -> 128 us  [the longest x4 67.3 us: shards(): arrived[chunk] = lax.ppermute(arrived[chunk], 'dp', ring)]
    all_to_all x6 -> x3, local copies, waits for them, and re-layouts: 75.9 us -> 2.52 us  [swap(): return lax.all_to_all(block, 'tp', split_axis=1, concat_axis=0, tiled=True)]
    dot_general x10 -> x13, matrix products: 116 us -> 46.7 us  [the longest x8 31.3 us: shards(): jnp.dot(blocks[chunk], out_block, preferred_element_type=jnp.float32)]
    all_gather x3 -> x1, local copies, waits for them, and re-layouts: 55 us -> 4.07 us  [gather(): return lax.all_gather(block, 'dp', axis=0, tiled=True)]
    all_to_all x1 -> x0, blocking collectives: 44.1 us -> none  [shards(): lax.all_to_all(out_cast, 'tp', split_axis=0, concat_axis=1, tiled=True)]
    pallas_call x0 -> x2, Pallas kernels: none -> 31.6 us  [attend(): pl.pallas_call(functools.partial(attention_kernel, heads, per_step, chunk...]
  transfers between devices with their start and end apart: 8 -> 18, of which waited for: 5 -> 12; matrix products, arithmetic and copies ran while one was open for 47% -> 21% of each run, Pallas kernels for 0% -> 6%
where the time goes in v2:
time: 573 us; the launch traced here: 566 us
  waiting for transfers between devices  302 us (53%)
  local copies, waits for them, and re-layouts  60.6 us (11%)
  matrix products  58.5 us (10%)
  blocking collectives  44.7 us (8%)
  Pallas kernels  31.6 us (6%)
  starting transfers between devices  27.5 us (5%)
  other arithmetic  21.8 us (4%)
  between operations  19.1 us (3%)
    all_gather x3, waiting for transfers between devices, gather(): return lax.all_gather(block, 'dp', axis=0, tiled=True)  77.3 us
    ppermute x4, waiting for transfers between devices, shards(): arrived[chunk] = lax.ppermute(arrived[chunk], 'dp', ring)  67.3 us
    reduce_scatter x2, waiting for transfers between devices, shards(): lax.psum_scatter(partial_out, 'tp', scatter_dimension=0, tiled=True)  49.9 us
    psum x1, blocking collectives, shards(): squares_total = lax.psum(local_squares, ('dp', 'tp'))  44.7 us
    ppermute x2, waiting for transfers between devices, shards(): pieces.append(lax.ppermute(reduced, ('dp', 'tp'), crossing))  38.2 us
    all_to_all x1, waiting for transfers between devices, shards(): lax.all_to_all(out_cast, 'tp', split_axis=0, concat_axis=1, tiled=True)  34.1 us
    pallas_call x2, Pallas kernels, attend(): pl.pallas_call(functools.partial(attention_kernel, heads, per_step, chunk...  31.6 us
    dot_general x8, matrix products, shards(): jnp.dot(blocks[chunk], out_block, preferred_element_type=jnp.float32)  31.3 us
  transfers between devices with their start and end apart: 18, of which 12 were waited for; matrix products, arithmetic and copies ran while one was open for 21% of the time, Pallas kernels for 6%

profile of v2, /device:TPU:2, one launch (start us, length us, event | category | flops | bytes accessed | tf_op | source)
XLA Modules:
  0.0 566.3 jit_solution(15285785026938351234)
XLA Ops:
  7.2 3.7 multiply_reduce_fusion.1
  10.9 1.1 copy.124
  12.0 3.5 all-to-all-start
  15.6 0.7 multiply_reduce_fusion.3
  16.3 13.2 %all-to-all-done = bf16[48,4,3072]{2,0,1:T(8,128)(2,1)S(1)} async-done(((bf16[48,4,3072]{2,0,1:T(8,128)(2,1)}), bf16[48,4,3072]{2,0,1:T(8,128)(2,1)S(1)}, u32[]{:S(2)}, u32[]{:S(2)}) %all-to-all-start) | async-done | bytes 1179680 | tf_op jit(solution)/shard_map/all_to_all | solution.py:140
  29.5 1.0 copy-done.10
  31.9 9.6 %multiply_reduce_fusion = (f32[]{:T(128)}, bf16[8192,224]{0,1:T(8,128)(2,1)}) fusion(f32[8192,224]{0,1:T(8,128)} %param.21), kind=kLoop, calls=%fused_computation.1 | loop fusion | flops 5505023 | bytes 11010052 | tf_op jit(solution)/shard_map/reduce_sum | solution.py:132
  42.2 5.0 all-to-all-start.1
  49.2 44.7 %psum.7 = f32[]{:T(128)} all-reduce(f32[]{:T(128)S(6)} %add.83), channel_id=1, replica_groups=mesh['dp'=8,'tp'=4] {'dp','tp'}, use_global_device_ids=true, to_apply=%region_4.0 | all-reduce | flops 1 | bytes 8 | tf_op jit(solution)/shard_map/psum | solution.py:134
  93.9 77.3 %all-gather.4.cloned.1.call-done = bf16[1536,3072]{1,0:T(8,128)(2,1)} async-done(((bf16[192,3072]{1,0:T(8,128)(2,1)}), bf16[1536,3072]{1,0:T(8,128)(2,1)}) %all-gather.4.cloned.1.call-update) | async-done | bytes 9437200 | tf_op jit(solution)/shard_map/all_gather | solution.py:143
  172.0 4.4 all-to-all-start.2
  176.3 4.3 copy.123
  181.4 6.3 %all-to-all-start.3 = ((bf16[4,2048,224]{1,2,0:T(8,128)(2,1)}), bf16[4,2048,224]{1,2,0:T(8,128)(2,1)}, u32[]{:S(2)}, u32[]{:S(2)}) async-start(bf16[4,2048,224]{1,2,0:T(8,128)(2,1)} %bitcast.107), calls=%async_computation.3 | async-start | bytes 7340032 | tf_op jit(solution)/shard_map/all_to_all | solution.py:156
  188.8 1.1 reshape_reshape.3
  189.9 1.1 copy.97
  192.5 2.2 multiply_cosine_fusion
  194.7 34.1 %all-to-all-done.3 = bf16[4,2048,224]{1,2,0:T(8,128)(2,1)} async-done(((bf16[4,2048,224]{1,2,0:T(8,128)(2,1)}), bf16[4,2048,224]{1,2,0:T(8,128)(2,1)}, u32[]{:S(2)}, u32[]{:S(2)}) %all-to-all-start.3) | async-done | bytes 3670048 | tf_op jit(solution)/shard_map/all_to_all | solution.py:156
  229.2 10.4 %convolution_convert_fusion.2 = bf16[512,3072]{1,0:T(8,128)(2,1)} fusion(bf16[512,1536]{1,0:T(8,128)(2,1)S(1)} %reshape_reshape.3, bf16[1536,3072]{1,0:T(8,128)(2,1)} %all-gather.4.cloned.1.call-done), kind=kOutput, calls=%fused_computation.3 | convolution fusion | flops 4833411072 | bytes 14155776 | tf_op jit(solution)/shard_map/dot_general | solution.py:187
  239.5 8.0 %reshape.115 = bf16[128,4,16,192]{3,2,1,0:T(8,128)(2,1)} reshape(bf16[512,3072]{1,0:T(8,128)(2,1)} %convolution_convert_fusion.2) | data formatting | bytes 6291456 | tf_op jit(solution)/shard_map/reshape | solution.py:190
  247.6 1.6 slice-done
  249.6 1.8 add_convert_fusion
  251.5 1.2 pad_maximum_fusion.1
  252.7 1.0 copy-done.8
  253.7 1.8 fusion.33
  255.5 4.4 copy.62
  259.9 3.5 convert_bitcast_fusion.1
  263.5 4.4 copy.65
  268.4 1.7 convert_bitcast_fusion
  270.1 2.4 copy.73
  272.5 15.8 %attend.3 = bf16[64,64,512]{2,1,0:T(8,128)(2,1)S(1)} custom-call(s32[128]{0:T(128)S(1)} %copy-done.6, bf16[64,64,512]{2,1,0:T(8,128)(2,1)S(1)} %bitcast.100, bf16[64,64,64]{2,1,0:T(8,128)(2,1)S(1)} %bitcast.104, bf16[128,256,512]{2,1,0:T(8,128)(2,1)} %cache_ref.3, bf16[128,64,256]{2,1,0:T(8,128)(2,1)S(1)} %copy-done.2, ...), custom_call_target="tpu_custom_call" | custom-call | flops 8589934592 | bytes 33554432 | tf_op jit(solution)/shard_map/attend/pallas_call | solution.py:102
  288.3 2.0 copy-done.5
  290.3 4.1 copy.61
  294.4 5.5 fusion.18
  301.0 1.1 copy-done.3
  302.1 15.9 %attend.2 = bf16[64,64,512]{2,1,0:T(8,128)(2,1)S(1)} custom-call(s32[128]{0:T(128)S(1)} %copy-done.6, bf16[64,64,512]{2,1,0:T(8,128)(2,1)S(1)} %bitcast.99, bf16[64,64,64]{2,1,0:T(8,128)(2,1)S(1)} %bitcast.103, bf16[128,256,512]{2,1,0:T(8,128)(2,1)} %cache_ref.3, bf16[128,64,256]{2,1,0:T(8,128)(2,1)S(1)} %copy-done.3, ...), custom_call_target="tpu_custom_call" | custom-call | flops 8589934592 | bytes 33554432 | tf_op jit(solution)/shard_map/attend/pallas_call | solution.py:102
  318.0 2.5 fusion.21
  321.3 1.2 copy.126
  323.2 5.1 collective-permute-done.5
  328.5 0.9 broadcast_in_dim.2
  329.4 2.6 constant_dynamic-update-slice_fusion.1
  332.0 17.3 %collective-permute-done = bf16[2048,896]{0,1:T(8,128)(2,1)} collective-permute-done((bf16[2048,896]{0,1:T(8,128)(2,1)}, bf16[2048,896]{0,1:T(8,128)(2,1)}, u32[]{:S(2)}, u32[]{:S(2)}) %collective-permute-start) | collective-permute-done | bytes 3670048 | tf_op jit(solution)/shard_map/ppermute | solution.py:166
  349.3 2.6 constant_dynamic-update-slice_fusion
  351.9 2.3 broadcast.50.clone
  354.2 3.2 fusion.7
  357.4 14.9 %collective-permute-done.6 = bf16[256,2048]{1,0:T(8,128)(2,1)S(1)} collective-permute-done((bf16[256,2048]{1,0:T(8,128)(2,1)}, bf16[256,2048]{1,0:T(8,128)(2,1)S(1)}, u32[]{:S(2)}, u32[]{:S(2)}) %collective-permute-start.6) | collective-permute-done | bytes 1048608 | tf_op jit(solution)/shard_map/ppermute | solution.py:244
  372.4 4.3 fusion.6
  376.6 3.0 fusion.5
  379.7 18.9 %collective-permute-done.7 = bf16[256,2048]{1,0:T(8,128)(2,1)S(1)} collective-permute-done((bf16[256,2048]{1,0:T(8,128)(2,1)S(1)}, bf16[256,2048]{1,0:T(8,128)(2,1)S(1)}, u32[]{:S(2)}, u32[]{:S(2)}) %collective-permute-start.7) | collective-permute-done | bytes 1048608 | tf_op jit(solution)/shard_map/ppermute | solution.py:244
  398.6 3.1 fusion.4
  401.9 2.1 broadcast.50.clone.1
  404.0 7.2 %fusion.11 = bf16[1024,1792]{1,0:T(8,128)(2,1)} fusion(bf16[1024,1792]{1,0:T(8,128)(2,1)} %broadcast.50.clone.1, s32[]{:T(128)S(6)} %select_n.30, bf16[2048,1792]{0,1:T(8,128)(2,1)} %copy-done.9, bf16[32,8,16,128]{3,2,1,0:T(8,128)(2,1)S(1)} %bitcast.115), kind=kOutput, calls=%fused_computation.28 | convolution fusion | flops 1879506944 | bytes 9306116 | tf_op jit(solution)/shard_map/dot_general | solution.py:236
  411.2 16.2 %collective-permute-done.2 = bf16[256,2048]{1,0:T(8,128)(2,1)S(1)} collective-permute-done((bf16[256,2048]{1,0:T(8,128)(2,1)}, bf16[256,2048]{1,0:T(8,128)(2,1)S(1)}, u32[]{:S(2)}, u32[]{:S(2)}) %collective-permute-start.2) | collective-permute-done | bytes 1048608 | tf_op jit(solution)/shard_map/ppermute | solution.py:244
  427.7 4.3 fusion.10
  432.0 3.0 fusion.9
  435.0 17.2 %collective-permute-done.3 = bf16[256,2048]{1,0:T(8,128)(2,1)S(1)} collective-permute-done((bf16[256,2048]{1,0:T(8,128)(2,1)S(1)}, bf16[256,2048]{1,0:T(8,128)(2,1)S(1)}, u32[]{:S(2)}, u32[]{:S(2)}) %collective-permute-start.3) | collective-permute-done | bytes 1048608 | tf_op jit(solution)/shard_map/ppermute | solution.py:244
  452.2 3.1 fusion.8
  455.4 1.9 collective-permute-start.8
  457.3 49.9 %reduce-scatter.3.cloned.1.call-done = bf16[256,1792]{1,0:T(8,128)(2,1)} async-done(((bf16[1024,1792]{1,0:T(8,128)(2,1)}), bf16[256,1792]{1,0:T(8,128)(2,1)}) %reduce-scatter.3.cloned.1.call-update) | async-done | bytes 917520 | tf_op jit(solution)/shard_map/reduce_scatter | solution.py:247
  507.2 4.0 collective-permute-start.4
  511.9 38.2 %collective-permute-done.4 = bf16[256,1792]{1,0:T(8,128)(2,1)} collective-permute-done((bf16[256,1792]{1,0:T(8,128)(2,1)}, bf16[256,1792]{1,0:T(8,128)(2,1)}, u32[]{:S(2)}, u32[]{:S(2)}) %collective-permute-start.4) | collective-permute-done | bytes 917536 | tf_op jit(solution)/shard_map/ppermute | solution.py:248
  550.2 1.3 pad_maximum_fusion
  551.5 2.2 reshape.128
  553.6 2.2 convolution_convert_fusion
  555.8 2.3 reshape.129
  (80 shorter events, 9.9 us)
Async XLA Ops:
  7.2 184.7 %copy-start = (bf16[128,4,64]{0,2,1:T(8,128)(2,1)S(1)}, bf16[128,4,64]{0,2,1:T(8,128)(2,1)}, u32[]{:S(2)}) copy-start(bf16[128,4,64]{0,2,1:T(8,128)(2,1)} %param.13) | copy-start | bytes 196612
  7.2 8.4 %copy-start.16 = (f32[16,8192]{1,0:T(8,128)S(1)}, f32[16,8192]{1,0:T(8,128)}, u32[]{:S(2)}) copy-start(f32[16,8192]{1,0:T(8,128)} %param.19) | copy-start | bytes 1572868
  12.0 17.5 %all-to-all-start = ((bf16[48,4,3072]{2,0,1:T(8,128)(2,1)}), bf16[48,4,3072]{2,0,1:T(8,128)(2,1)S(1)}, u32[]{:S(2)}, u32[]{:S(2)}) async-start(bf16[48,4,3072]{2,0,1:T(8,128)(2,1)} %bitcast.93), calls=%async_computation | async-start | bytes 2359296 | tf_op jit(solution)/shard_map/all_to_all | solution.py:140
  15.5 155.7 %all-gather.4.cloned.1.call-start = ((), (), s32[]{:S(2)}) async-start(), calls=%async_computation.6 | async-start | bytes 10616832 | tf_op jit(solution)/shard_map/all_gather | solution.py:143
  29.5 1.0 copy-start.10
  31.9 15.3 %copy-start.17 = (f32[16,8192]{1,0:T(8,128)S(1)}, f32[16,8192]{1,0:T(8,128)}, u32[]{:S(2)}) copy-start(f32[16,8192]{1,0:T(8,128)} %param.20) | copy-start | bytes 1572868
  42.2 51.7 %all-to-all-start.1 = ((bf16[16,4,2048]{2,0,1:T(8,128)(2,1)}), bf16[16,4,2048]{2,0,1:T(8,128)(2,1)S(1)}, u32[]{:S(2)}, u32[]{:S(2)}) async-start(bf16[16,4,2048]{2,0,1:T(8,128)(2,1)} %bitcast.97), calls=%async_computation.1 | async-start | bytes 524288 | tf_op jit(solution)/shard_map/all_to_all | solution.py:140
  47.2 181.6 %all-gather.6.cloned.1.call-start = ((), (), s32[]{:S(2)}) async-start(), calls=%async_computation.7 | async-start | bytes 2359296 | tf_op jit(solution)/shard_map/all_gather | solution.py:143
  93.9 77.3 %copy-start.15 = (bf16[16,4,2048]{2,0,1:T(8,128)(2,1)}, bf16[16,4,2048]{2,0,1:T(8,128)(2,1)S(1)}, u32[]{:S(2)}) copy-start(bf16[16,4,2048]{2,0,1:T(8,128)(2,1)S(1)} %all-to-all-done.1) | copy-start | bytes 786436
  172.0 8.8 %all-to-all-start.2 = ((bf16[16,4,2048]{2,0,1:T(8,128)(2,1)}), bf16[16,4,2048]{2,0,1:T(8,128)(2,1)S(1)}, u32[]{:S(2)}, u32[]{:S(2)}) async-start(bf16[16,4,2048]{2,0,1:T(8,128)(2,1)} %bitcast.96), calls=%async_computation.2 | async-start | bytes 524288 | tf_op jit(solution)/shard_map/all_to_all | solution.py:140
  180.7 0.7 copy-start.14
  180.7 7.1 %copy-start.13 = (bf16[128,4,1536]{2,1,0:T(4,128)(2,1)S(1)}, bf16[128,4,1536]{2,1,0:T(4,128)(2,1)}, u32[]{:S(2)}) copy-start(bf16[128,4,1536]{2,1,0:T(4,128)(2,1)} %param.11) | copy-start | bytes 4718596
  180.7 7.4 %copy-start.18 = (s32[1,128]{1,0:T(1,128)S(1)}, s32[1,128]{1,0:T(1,128)}, u32[]{:S(2)}) copy-start(s32[1,128]{1,0:T(1,128)} %param.17) | copy-start | bytes 1540
  181.4 47.3 %all-to-all-start.3 = ((bf16[4,2048,224]{1,2,0:T(8,128)(2,1)}), bf16[4,2048,224]{1,2,0:T(8,128)(2,1)}, u32[]{:S(2)}, u32[]{:S(2)}) async-start(bf16[4,2048,224]{1,2,0:T(8,128)(2,1)} %bitcast.107), calls=%async_computation.3 | async-start | bytes 7340032 | tf_op jit(solution)/shard_map/all_to_all | solution.py:156
  187.8 102.5 %all-gather.8.cloned.1.call-start = ((), (), s32[]{:S(2)}) async-start(), calls=%async_computation.8 | async-start | bytes 2359296 | tf_op jit(solution)/shard_map/all_gather | solution.py:143
  188.8 3.6 copy-start.6
  228.8 226.6 %reduce-scatter.5.cloned.1.call-start = ((), (), s32[]{:S(2)}) async-start(), calls=%async_computation.10 | async-start | bytes 4587520 | tf_op jit(solution)/shard_map/reduce_scatter | solution.py:247
  247.6 1.6 slice-start
  251.5 2.2 copy-start.8
  263.4 5.0 copy-start.7
  263.5 5.0 copy-start.11
  267.8 81.5 %collective-permute-start = (bf16[2048,896]{0,1:T(8,128)(2,1)}, bf16[2048,896]{0,1:T(8,128)(2,1)}, u32[]{:S(2)}, u32[]{:S(2)}) collective-permute-start(bf16[2048,896]{0,1:T(8,128)(2,1)} %bitcast.8), channel_id=1, source_target_pairs={{0,4},{4,0},{8,12},{12,8},{16,20},{20,16},{24,28},{28,24},{1,5},{5... | collective-permute-start | bytes 11010056 | tf_op jit(solution)/shard_map/ppermute | solution.py:166
  270.1 2.4 copy-start.2
  288.3 2.0 copy-start.5
  294.4 6.6 %copy-start.4 = (bf16[64,4,16,512]{3,2,1,0:T(8,128)(2,1)S(1)}, bf16[64,4,16,512]{3,2,1,0:T(8,128)(2,1)}, u32[]{:S(2)}) copy-start(bf16[64,4,16,512]{3,2,1,0:T(8,128)(2,1)} %copy.65) | copy-start | bytes 12582916
  299.9 2.2 copy-start.3
  300.9 27.3 %collective-permute-start.5 = (bf16[256,2048]{1,0:T(8,128)(2,1)S(1)}, bf16[256,2048]{1,0:T(8,128)(2,1)}, u32[]{:S(2)}, u32[]{:S(2)}) collective-permute-start(bf16[256,2048]{1,0:T(8,128)(2,1)S(1)} %bitcast.121), channel_id=1, source_target_pairs={{0,8},{4,12},{8,16},{12,20},{16,24},{20,28},{24,0},{28,4},{1,9},{5... | collective-permute-start | bytes 3145736 | tf_op jit(solution)/shard_map/ppermute | solution.py:231
  302.1 15.9 %copy-start.12 = (bf16[512,2048]{0,1:T(8,128)(2,1)S(1)}, bf16[512,2048]{0,1:T(8,128)(2,1)}, u32[]{:S(2)}) copy-start(bf16[512,2048]{0,1:T(8,128)(2,1)} %copy.61) | copy-start | bytes 6291460
  322.5 29.4 %collective-permute-start.1 = (bf16[256,2048]{1,0:T(8,128)(2,1)}, bf16[256,2048]{1,0:T(8,128)(2,1)}, u32[]{:S(2)}, u32[]{:S(2)}) collective-permute-start(bf16[256,2048]{1,0:T(8,128)(2,1)} %bitcast.95), channel_id=1, source_target_pairs={{0,8},{4,12},{8,16},{12,20},{16,24},{20,28},{24,0},{28,4},{1,9},{5... | collective-permute-start | bytes 3145736 | tf_op jit(solution)/shard_map/ppermute | solution.py:231
  328.3 44.1 %collective-permute-start.6 = (bf16[256,2048]{1,0:T(8,128)(2,1)}, bf16[256,2048]{1,0:T(8,128)(2,1)S(1)}, u32[]{:S(2)}, u32[]{:S(2)}) collective-permute-start(bf16[256,2048]{1,0:T(8,128)(2,1)} %collective-permute-done.5), channel_id=1, source_target_pairs={{0,8},{4,12},{8,16},{12,20},{16,24},{20,28},{24,0},{28,4},{1,9},{5... | collective-permute-start | bytes 3145736 | tf_op jit(solution)/shard_map/ppermute | solution.py:244
  351.9 46.8 %copy-start.9 = (bf16[2048,1792]{0,1:T(8,128)(2,1)}, bf16[2048,1792]{0,1:T(8,128)(2,1)S(1)}, u32[]{:S(2)}) copy-start(bf16[2048,1792]{0,1:T(8,128)(2,1)S(1)} %constant_dynamic-update-slice_fusion) | copy-start | bytes 22020100
  372.4 26.3 %collective-permute-start.7 = (bf16[256,2048]{1,0:T(8,128)(2,1)S(1)}, bf16[256,2048]{1,0:T(8,128)(2,1)S(1)}, u32[]{:S(2)}, u32[]{:S(2)}) collective-permute-start(bf16[256,2048]{1,0:T(8,128)(2,1)S(1)} %collective-permute-done.6), channel_id=1, source_target_pairs={{0,8},{4,12},{8,16},{12,20},{16,24},{20,28},{24,0},{28,4},{1,9},{5... | collective-permute-start | bytes 3145736 | tf_op jit(solution)/shard_map/ppermute | solution.py:244
  401.7 105.5 %reduce-scatter.3.cloned.1.call-start = ((), (), s32[]{:S(2)}) async-start(), calls=%async_computation.9 | async-start | bytes 4587520 | tf_op jit(solution)/shard_map/reduce_scatter | solution.py:247
  401.8 25.7 %collective-permute-start.2 = (bf16[256,2048]{1,0:T(8,128)(2,1)}, bf16[256,2048]{1,0:T(8,128)(2,1)S(1)}, u32[]{:S(2)}, u32[]{:S(2)}) collective-permute-start(bf16[256,2048]{1,0:T(8,128)(2,1)} %collective-permute-done.1), channel_id=1, source_target_pairs={{0,8},{4,12},{8,16},{12,20},{16,24},{20,28},{24,0},{28,4},{1,9},{5... | collective-permute-start | bytes 3145736 | tf_op jit(solution)/shard_map/ppermute | solution.py:244
  401.9 25.8 %slice-start.1 = ((s8[7340032]{0:T(1024)(128)(4,1)}), s8[4194304]{0:T(1024)(128)(4,1)S(1)}, s32[]{:S(2)}) async-start(s8[7340032]{0:T(1024)(128)(4,1)} %bitcast.109), calls=%async_computation.12 | async-start | bytes 8388608
  404.0 23.7 %slice-start.2 = ((s8[7340032]{0:T(1024)(128)(4,1)}), s8[3145728]{0:T(1024)(128)(4,1)S(1)}, s32[]{:S(2)}) async-start(s8[7340032]{0:T(1024)(128)(4,1)} %bitcast.109), calls=%async_computation.13 | async-start | bytes 6291456
  427.5 24.8 %collective-permute-start.3 = (bf16[256,2048]{1,0:T(8,128)(2,1)S(1)}, bf16[256,2048]{1,0:T(8,128)(2,1)S(1)}, u32[]{:S(2)}, u32[]{:S(2)}) collective-permute-start(bf16[256,2048]{1,0:T(8,128)(2,1)S(1)} %collective-permute-done.2), channel_id=1, source_target_pairs={{0,8},{4,12},{8,16},{12,20},{16,24},{20,28},{24,0},{28,4},{1,9},{5... | collective-permute-start | bytes 3145736 | tf_op jit(solution)/shard_map/ppermute | solution.py:244
  455.4 56.6 %collective-permute-start.8 = (bf16[256,1792]{1,0:T(8,128)(2,1)}, bf16[256,1792]{1,0:T(8,128)(2,1)S(1)}, u32[]{:S(2)}, u32[]{:S(2)}) collective-permute-start(bf16[256,1792]{1,0:T(8,128)(2,1)} %reduce-scatter.5.cloned.1.call-done), channel_id=1, source_target_pairs={{0,0},{1,8},{2,16},{3,24},{4,4},{5,12},{6,20},{7,28},{8,1},{9,9},{... | collective-permute-start | bytes 2752520 | tf_op jit(solution)/shard_map/ppermute | solution.py:248
  507.2 42.9 %collective-permute-start.4 = (bf16[256,1792]{1,0:T(8,128)(2,1)}, bf16[256,1792]{1,0:T(8,128)(2,1)}, u32[]{:S(2)}, u32[]{:S(2)}) collective-permute-start(bf16[256,1792]{1,0:T(8,128)(2,1)} %reduce-scatter.3.cloned.1.call-done), channel_id=1, source_target_pairs={{0,0},{1,8},{2,16},{3,24},{4,4},{5,12},{6,20},{7,28},{8,1},{9,9},{... | collective-permute-start | bytes 2752520 | tf_op jit(solution)/shard_map/ppermute | solution.py:248
  551.5 6.7 %copy-start.1 = (bf16[128,4,64]{0,2,1:T(8,128)(2,1)S(1)}, bf16[128,4,64]{0,2,1:T(8,128)(2,1)}, u32[]{:S(2)}) copy-start(bf16[128,4,64]{0,2,1:T(8,128)(2,1)} %param.13) | copy-start | bytes 196612
Sparse Core Ops, SparseCore 0:
  30.7 140.4 all-gather.3
  173.3 47.5 all-gather.5
  228.9 47.2 all-gather.7
  401.9 38.2 reduce-scatter.4
  455.5 51.6 reduce-scatter.2
